TPU v7x, 128 devices: a whole 4x4x4 slice. The times are simulated.
128 devices in a mesh: row: 16 (over z, y_hi, core), col: 8 (over y_lo, x).
Axes of the slice: x: 4, y: 4 (y_hi: 2, y_lo: 2; y = y_hi * 2 + y_lo), z: 4, core: 2. Of those that a mesh axis runs over, the one named last changes fastest.
Arguments:
- left_prop: float32 [16, 8, 2, 512, 512], P('row', None, None, 'col'), may hold values from -0.1875 to 0.1875
- vertex: float32 [8, 2, 512, 512], P(None, None, ('row', 'col')), may hold values from -5 to 5
- right_prop: float32 [8, 16, 2, 512, 512], P(None, 'col', None, None, 'row'), may hold values from -0.1875 to 0.1875
- insertions: int32 [3], replicated, may hold values from 0 to 7
- window_start: int32 [2], replicated, may hold values from 0 to 255
Outputs:
- correlator: float32 [16, 16, 2, 512, 512], P('row', 'col')
Inputs may be any that keep to these rules, and one draw needn't show every extreme that they name: `insertions`: repeats may occur.
All inputs are finite; a program needn't handle non-finite values.
Results may differ from a plain program's by a relative error of at most 0.0001.
Values sent between devices are 32-bit elements; how exact they have to be, the bound alone decides.
No kernel may reach another device: no remote copies, remote signals or barrier semaphores. Data moves between devices by JAX's collectives and lax.ppermute only.
A program may use at most 128 MiB of HBM per device.

v0:
```python
import jax
import jax.numpy as jnp
from jax import lax
from jax.sharding import Mesh
from jax.sharding import PartitionSpec as P

NS = 8
LT = 256
ROW = ("row_0", "row_1", "row_2")
COL = ("col_0", "col_1")
ROW_COL = ("row_0", "row_1", "row_2", "col_0", "col_1")


def piece_ends(length, count):
    unit = 8 if length >= 8 * count else 1
    return [length // unit * k // count * unit for k in range(1, count)]


def all_blocks(x, axes, order):
    tiles = x[None]
    for k in order:
        tiles = lax.all_gather(tiles, axes[k], axis=0, tiled=True)
    held = [lax.axis_size(axes[k]) for k in reversed(order)]
    tiles = tiles.reshape(*held, *x.shape)
    turned = sorted(range(len(order)), key=lambda place: order[len(order) - 1 - place])
    return tiles.transpose(*turned, *range(len(order), tiles.ndim)).reshape(-1, *x.shape)


def in_order(tiles, dim):
    shape = list(tiles.shape[1:])
    shape[dim] *= tiles.shape[0]
    return jnp.moveaxis(tiles, 0, dim).reshape(shape)


def spread_gather(x, axes, dim):
    cut = max(range(max(1, x.ndim - 1)), key=lambda d: x.shape[d])
    count, finished = (len(axes), [])
    for leading, share in enumerate(jnp.split(x, piece_ends(x.shape[cut], count), axis=cut)):
        if share.size:
            order = [(leading - k) % count for k in range(count)]
            finished.append(all_blocks(share, axes, order))
    return in_order(jnp.concatenate(finished, axis=cut + 1), dim)


def complex_product(first, second):
    highest = lax.Precision.HIGHEST
    first_re, first_im = (first[..., 0, :, :], first[..., 1, :, :])
    second_re, second_im = (second[..., 0, :, :], second[..., 1, :, :])
    real_part = jnp.matmul(first_re, second_re, precision=highest) - jnp.matmul(
        first_im, second_im, precision=highest
    )
    imag_part = jnp.matmul(first_re, second_im, precision=highest) + jnp.matmul(
        first_im, second_re, precision=highest
    )
    return jnp.stack([real_part, imag_part], axis=-3)


def contract_with(left_operand, column_piece):
    summed = complex_product(left_operand[:, 0, None], column_piece[0][None])
    for which in range(1, column_piece.shape[0]):
        summed = summed + complex_product(left_operand[:, which, None], column_piece[which][None])
    return summed


def per_device(left_prop, vertex, right_prop, insertions, window_start):
    source_count = left_prop.shape[0]
    sink_count = right_prop.shape[1]
    source_slots = lax.axis_index(ROW) * source_count + jnp.arange(source_count, dtype=jnp.int32)
    sink_slots = lax.axis_index(COL) * sink_count + jnp.arange(sink_count, dtype=jnp.int32)
    slice_times = insertions * (LT // NS)
    source_times = (window_start[0] + source_slots) % LT
    sink_times = (window_start[1] + sink_slots) % LT
    left_sign = jnp.where(slice_times[None, :] < source_times[:, None], -1.0, 1.0).astype(
        jnp.float32
    )
    right_sign = jnp.where(sink_times[None, :] < slice_times[:, None], -1.0, 1.0).astype(
        jnp.float32
    )
    chosen_left = jnp.take(left_prop, insertions, axis=1) * left_sign[:, :, None, None, None]
    chosen_right = jnp.take(right_prop, insertions, axis=0) * right_sign[:, :, None, None, None]
    vertex_part = jnp.take(vertex, insertions, axis=0)
    vertex_full = spread_gather(vertex_part, ROW_COL, 2)
    left_full = lax.all_gather(chosen_left, COL, axis=3, tiled=True)
    vertex_right = complex_product(vertex_full[:, None], chosen_right)
    result = contract_with(left_full, lax.all_gather(vertex_right, ROW, axis=4, tiled=True))
    return result


def solution(mesh):
    finer = Mesh(mesh.devices.reshape(4, 2, 2, 2, 4), ("row_0", "row_1", "row_2", "col_0", "col_1"))
    return jax.shard_map(
        per_device,
        mesh=finer,
        in_specs=(
            P(ROW, None, None, COL, None),
            P(None, None, ROW_COL, None),
            P(None, COL, None, None, ROW),
            P(),
            P(),
        ),
        out_specs=P(ROW, COL, None, None, None),
        check_vma=False,
    )
```

profile of v0, /device:TPU:1, one launch (start us, length us, event | category | flops | bytes accessed | tf_op | source)
XLA Modules:
  0.0 401.7 jit_solution(11193293117327762396)
XLA Ops:
  9.6 5.5 %all-gather = f32[6,2,1,512]{3,1,2,0:T(2,128)S(1)} all-gather(f32[3,2,1,512]{3,1,2,0:T(2,128)S(1)} %copy.62), channel_id=2, replica_groups=mesh['row_0'=4,'row_1'=2,'row_2'=2,'col_0'=2,'col_1'=4] {'row_1'}, dimensions={0}, use_global_device_ids=true | all-gather | bytes 36864 | tf_op jit(solution)/shard_map/all_gather | solution.py:22
  15.1 10.3 %all_gather.68 = f32[8,3,2,1,512]{4,2,3,1,0:T(2,128)S(1)} all-gather(f32[2,3,2,1,512]{4,2,3,1,0:T(2,128)S(1)} %bitcast.186), channel_id=1, replica_groups=mesh['row_0'=4,'row_1'=2,'row_2'=2,'col_0'=2,'col_1'=4] {'row_0'}, dimensions={0}, use_global_device_ids=true | all-gather | bytes 122880 | tf_op jit(solution)/shard_map/all_gather | solution.py:22
  25.4 10.4 %all_gather.69 = f32[32,3,2,1,512]{4,2,3,1,0:T(2,128)S(1)} all-gather(f32[8,3,2,1,512]{4,2,3,1,0:T(2,128)S(1)} %all_gather.68), channel_id=1, replica_groups=mesh['row_0'=4,'row_1'=2,'row_2'=2,'col_0'=2,'col_1'=4] {'col_1'}, dimensions={0}, use_global_device_ids=true | all-gather | bytes 491520 | tf_op jit(solution)/shard_map/all_gather | solution.py:22
  35.9 7.4 %all_gather.70 = f32[64,3,2,1,512]{4,2,3,1,0:T(2,128)} all-gather(f32[32,3,2,1,512]{4,2,3,1,0:T(2,128)S(1)} %all_gather.69), channel_id=1, replica_groups=mesh['row_0'=4,'row_1'=2,'row_2'=2,'col_0'=2,'col_1'=4] {'col_0'}, dimensions={0}, use_global_device_ids=true | all-gather | bytes 1179648 | tf_op jit(solution)/shard_map/all_gather | solution.py:22
  43.4 9.9 %all-gather.1 = f32[6,2,1,512]{3,1,2,0:T(2,128)S(1)} all-gather(f32[3,2,1,512]{3,1,2,0:T(2,128)S(1)} %copy.65), channel_id=3, replica_groups=mesh['row_0'=4,'row_1'=2,'row_2'=2,'col_0'=2,'col_1'=4] {'row_2'}, dimensions={0}, use_global_device_ids=true | all-gather | bytes 36864 | tf_op jit(solution)/shard_map/all_gather | solution.py:22
  53.3 4.8 %all_gather.73 = f32[4,3,2,1,512]{4,2,3,1,0:T(2,128)S(1)} all-gather(f32[2,3,2,1,512]{4,2,3,1,0:T(2,128)S(1)} %bitcast.184), channel_id=1, replica_groups=mesh['row_0'=4,'row_1'=2,'row_2'=2,'col_0'=2,'col_1'=4] {'row_1'}, dimensions={0}, use_global_device_ids=true | all-gather | bytes 73728 | tf_op jit(solution)/shard_map/all_gather | solution.py:22
  58.1 9.2 %all_gather.74 = f32[16,3,2,1,512]{4,2,3,1,0:T(2,128)S(1)} all-gather(f32[4,3,2,1,512]{4,2,3,1,0:T(2,128)S(1)} %all_gather.73), channel_id=1, replica_groups=mesh['row_0'=4,'row_1'=2,'row_2'=2,'col_0'=2,'col_1'=4] {'row_0'}, dimensions={0}, use_global_device_ids=true | all-gather | bytes 245760 | tf_op jit(solution)/shard_map/all_gather | solution.py:22
  67.4 11.5 %all_gather.75 = f32[64,3,2,1,512]{4,2,3,1,0:T(2,128)} all-gather(f32[16,3,2,1,512]{4,2,3,1,0:T(2,128)S(1)} %all_gather.74), channel_id=1, replica_groups=mesh['row_0'=4,'row_1'=2,'row_2'=2,'col_0'=2,'col_1'=4] {'col_1'}, dimensions={0}, use_global_device_ids=true | all-gather | bytes 983040 | tf_op jit(solution)/shard_map/all_gather | solution.py:22
  82.5 9.5 %all_gather.78 = f32[4,3,2,1,512]{4,2,3,1,0:T(2,128)S(1)} all-gather(f32[2,3,2,1,512]{4,2,3,1,0:T(2,128)S(1)} %bitcast.185), channel_id=1, replica_groups=mesh['row_0'=4,'row_1'=2,'row_2'=2,'col_0'=2,'col_1'=4] {'row_2'}, dimensions={0}, use_global_device_ids=true | all-gather | bytes 73728 | tf_op jit(solution)/shard_map/all_gather | solution.py:22
  92.1 5.1 %all_gather.79 = f32[8,3,2,1,512]{4,2,3,1,0:T(2,128)S(1)} all-gather(f32[4,3,2,1,512]{4,2,3,1,0:T(2,128)S(1)} %all_gather.78), channel_id=1, replica_groups=mesh['row_0'=4,'row_1'=2,'row_2'=2,'col_0'=2,'col_1'=4] {'row_1'}, dimensions={0}, use_global_device_ids=true | all-gather | bytes 147456 | tf_op jit(solution)/shard_map/all_gather | solution.py:22
  97.2 10.7 %all_gather.80 = f32[32,3,2,1,512]{4,2,3,1,0:T(2,128)} all-gather(f32[8,3,2,1,512]{4,2,3,1,0:T(2,128)S(1)} %all_gather.79), channel_id=1, replica_groups=mesh['row_0'=4,'row_1'=2,'row_2'=2,'col_0'=2,'col_1'=4] {'row_0'}, dimensions={0}, use_global_device_ids=true | all-gather | bytes 491520 | tf_op jit(solution)/shard_map/all_gather | solution.py:22
  108.0 9.1 %all-gather.3 = f32[12,2,1,512]{3,1,2,0:T(2,128)S(1)} all-gather(f32[3,2,1,512]{3,1,2,0:T(2,128)S(1)} %copy.71), channel_id=5, replica_groups=mesh['row_0'=4,'row_1'=2,'row_2'=2,'col_0'=2,'col_1'=4] {'col_1'}, dimensions={0}, use_global_device_ids=true | all-gather | bytes 61440 | tf_op jit(solution)/shard_map/all_gather | solution.py:22
  117.2 3.9 all_gather.83
  121.1 9.2 %all_gather.84 = f32[16,3,2,1,512]{4,3,0,1,2:T(1,128)S(1)} all-gather(f32[8,3,2,1,512]{4,3,0,1,2:T(1,128)S(1)} %all_gather.83), channel_id=1, replica_groups=mesh['row_0'=4,'row_1'=2,'row_2'=2,'col_0'=2,'col_1'=4] {'row_2'}, dimensions={0}, use_global_device_ids=true | all-gather | bytes 294912 | tf_op jit(solution)/shard_map/all_gather | solution.py:22
  130.3 9.6 %all_gather.85 = f32[32,3,2,1,512]{4,3,0,1,2:T(1,128)} all-gather(f32[16,3,2,1,512]{4,3,0,1,2:T(1,128)S(1)} %all_gather.84), channel_id=1, replica_groups=mesh['row_0'=4,'row_1'=2,'row_2'=2,'col_0'=2,'col_1'=4] {'row_1'}, dimensions={0}, use_global_device_ids=true | all-gather | bytes 589824 | tf_op jit(solution)/shard_map/all_gather | solution.py:22
  149.7 3.7 reshape.208
  157.0 4.3 %reshape.210 = f32[128,3,2,1,512]{4,3,0,1,2:T(1,128)} reshape(f32[4,2,2,2,4,3,2,1,512]{8,4,3,2,1,0,5,6,7:T(4,128)} %copy.67) | data formatting | bytes 3145728 | tf_op jit(solution)/shard_map/reshape | solution.py:26
  164.9 4.2 %reshape.212 = f32[128,3,2,1,512]{4,3,0,1,2:T(1,128)} reshape(f32[4,2,2,2,4,3,2,1,512]{8,4,3,2,1,0,5,6,7:T(4,128)} %copy.70) | data formatting | bytes 3145728 | tf_op jit(solution)/shard_map/reshape | solution.py:26
  169.1 3.9 all-gather.19.cloned.1.call-done
  173.0 8.6 %maximum_bitcast_fusion = f32[3,2,128,4,512]{4,3,2,0,1:T(4,128)} fusion(f32[128,3,2,1,512]{4,3,0,1,2:T(1,128)} %all-gather.19.cloned.1.call-done, f32[128,3,2,1,512]{4,3,0,1,2:T(1,128)} %reshape.212, f32[128,3,2,1,512]{4,3,0,1,2:T(1,128)} %reshape.210, f32[128,3,2,1,512]{4,3,0,1,2:T(1,128)S(1)} %reshape.208), kind=kLoop, calls=%fused_computation.3 | loop fusion | flops 4718592 | bytes 12582912 | tf_op jit(solution)/shard_map/transpose | solution.py:32
  181.6 8.2 %broadcast_in_dim_reshape.3 = f32[3,1,2,512,512]{4,3,0,2,1:T(8,128)} reshape(f32[3,2,128,4,512]{4,3,2,0,1:T(4,128)} %maximum_bitcast_fusion) | data formatting | bytes 12582912 | tf_op jit(solution)/shard_map/broadcast_in_dim;reshape | solution.py:84
  189.8 5.2 %fusion.1 = f32[3,512,64]{1,2,0:S(1)} fusion(f32[3,512,64]{1,2,0:T(8,128)S(1)} %bitcast.174, f32[3,1,2,512,512]{4,3,0,2,1:T(8,128)} %broadcast_in_dim_reshape.3), kind=kOutput, calls=%fused_computation.8 | convolution fusion | flops 603979776 | bytes 3932160
  195.1 5.1 %fusion.4 = f32[3,512,64]{1,2,0:S(1)} fusion(f32[3,512,64]{1,2,0:T(8,128)S(1)} %bitcast.175, f32[3,1,2,512,512]{4,3,0,2,1:T(8,128)} %broadcast_in_dim_reshape.3), kind=kOutput, calls=%fused_computation.11 | convolution fusion | flops 603979776 | bytes 3932160
  207.6 38.9 %all-gather.11.cloned.1.call-done = f32[1,3,2,512,512]{4,3,2,1,0:T(8,128)} async-done(((f32[1,3,2,64,512]{4,3,2,1,0:T(8,128)}), f32[1,3,2,512,512]{4,3,2,1,0:T(8,128)}) %all-gather.11.cloned.1.call-update) | async-done | bytes 6291472 | tf_op jit(solution)/shard_map/all_gather | solution.py:83
  246.5 92.3 %all-gather.21.cloned.1.call-done = f32[3,2,2,512,512]{3,4,1,0,2:T(8,128)} async-done(((f32[3,2,2,512,32]{3,4,1,0,2:T(8,128)}), f32[3,2,2,512,512]{3,4,1,0,2:T(8,128)}) %all-gather.21.cloned.1.call-update) | async-done | bytes 12582928 | tf_op jit(solution)/shard_map/all_gather | solution.py:85
  338.9 5.8 %fusion.13 = f32[512,2,512]{2,0,1:T(8,128)S(1)} fusion(f32[3,2,2,512,512]{3,4,1,0,2:T(8,128)} %all-gather.21.cloned.1.call-done, f32[1,3,2,512,512]{4,3,2,1,0:T(8,128)} %all-gather.11.cloned.1.call-done), kind=kOutput, calls=%fused_computation.32 | convolution fusion | flops 3221225472 | bytes 5242880 | tf_op jit(solution)/shard_map/dot_general | solution.py:52
  344.7 5.5 %fusion.9 = f32[512,2,512]{2,0,1:T(8,128)S(1)} fusion(f32[3,2,2,512,512]{3,4,1,0,2:T(8,128)} %all-gather.21.cloned.1.call-done, f32[1,3,2,512,512]{4,3,2,1,0:T(8,128)} %all-gather.11.cloned.1.call-done), kind=kOutput, calls=%fused_computation.28 | convolution fusion | flops 3221225472 | bytes 5242880 | tf_op jit(solution)/shard_map/dot_general | solution.py:52
  350.2 5.6 %fusion.5 = f32[512,2,512]{2,0,1:T(8,128)S(1)} fusion(f32[3,2,2,512,512]{3,4,1,0,2:T(8,128)} %all-gather.21.cloned.1.call-done, f32[1,3,2,512,512]{4,3,2,1,0:T(8,128)} %all-gather.11.cloned.1.call-done), kind=kOutput, calls=%fused_computation.24 | convolution fusion | flops 3221225472 | bytes 5242880 | tf_op jit(solution)/shard_map/dot_general | solution.py:52
  355.9 5.1 %fusion.14 = f32[512,2,512]{2,0,1:T(8,128)S(1)} fusion(f32[3,2,2,512,512]{3,4,1,0,2:T(8,128)S(1)} %copy-done.3, f32[1,3,2,512,512]{4,3,2,1,0:T(8,128)} %all-gather.11.cloned.1.call-done), kind=kOutput, calls=%fused_computation.33 | convolution fusion | flops 3221225472 | bytes 5242880 | tf_op jit(solution)/shard_map/dot_general | solution.py:49
  371.7 4.0 %add_bitcast_fusion.1 = f32[1,2,1,512,512]{4,3,1,2,0:T(8,128)S(1)} fusion(f32[512,2,512]{2,0,1:T(8,128)S(1)} %fusion.9, f32[3,2,2,512,512]{3,4,1,0,2:T(8,128)S(1)} %copy-done.3, f32[1,3,2,512,512]{4,3,2,1,0:T(8,128)S(1)} %copy-done.4), kind=kOutput, calls=%fused_computation.20 | convolution fusion | flops 3221749760 | bytes 7340032 | tf_op jit(solution)/shard_map/dot_general | solution.py:52
  383.0 3.8 subtract_bitcast_fusion.1
  386.8 3.7 subtract_bitcast_fusion.2
  (64 shorter events, 52.6 us)
Async XLA Ops:
  6.5 134.7 %copy-start = (f32[1,8,2,64,512]{4,3,2,1,0:T(8,128)S(1)}, f32[1,8,2,64,512]{4,3,2,1,0:T(8,128)}, u32[]{:S(2)}) copy-start(f32[1,8,2,64,512]{4,3,2,1,0:T(8,128)} %param.5) | copy-start | bytes 6291460
  6.5 139.6 %all-gather.13.cloned.1.call-start = ((), (), s32[]{:S(2)}) async-start(), calls=%async_computation.1 | async-start | bytes 2359296 | tf_op jit(solution)/shard_map/all_gather | solution.py:22
  43.3 96.7 %copy-start.5 = (s32[2]{0:T(128)S(1)}, s32[2]{0:T(128)}, u32[]{:S(2)}) copy-start(s32[2]{0:T(128)} %param.9) | copy-start | bytes 28
  43.3 110.1 %all-gather.15.cloned.1.call-start = ((), (), s32[]{:S(2)}) async-start(), calls=%async_computation.2 | async-start | bytes 2359296 | tf_op jit(solution)/shard_map/all_gather | solution.py:22
  67.4 74.5 %copy-start.6 = (s32[3]{0:T(128)S(1)}, s32[3]{0:T(128)}, u32[]{:S(2)}) copy-start(s32[3]{0:T(128)} %param.8) | copy-start | bytes 40
  78.8 82.4 %all-gather.17.cloned.1.call-start = ((), (), s32[]{:S(2)}) async-start(), calls=%async_computation.3 | async-start | bytes 1966080 | tf_op jit(solution)/shard_map/all_gather | solution.py:22
  107.9 65.1 %all-gather.19.cloned.1.call-start = ((), (), s32[]{:S(2)}) async-start(), calls=%async_computation.4 | async-start | bytes 1966080 | tf_op jit(solution)/shard_map/all_gather | solution.py:22
  139.9 106.6 %all-gather.11.cloned.1.call-start = ((), (), s32[]{:S(2)}) async-start(), calls=%async_computation | async-start | bytes 7077888 | tf_op jit(solution)/shard_map/all_gather | solution.py:83
  142.9 195.9 %all-gather.21.cloned.1.call-start = ((), (), s32[]{:S(2)}) async-start(), calls=%async_computation.5 | async-start | bytes 13369344 | tf_op jit(solution)/shard_map/all_gather | solution.py:85
  189.8 10.3 %copy-start.2 = (f32[3,1,2,512,512]{4,3,0,2,1:T(8,128)S(1)}, f32[3,1,2,512,512]{4,3,0,2,1:T(8,128)}, u32[]{:S(2)}) copy-start(f32[3,1,2,512,512]{4,3,0,2,1:T(8,128)} %broadcast_in_dim_reshape.3) | copy-start | bytes 18874372
  338.9 17.0 %copy-start.3 = (f32[3,2,2,512,512]{3,4,1,0,2:T(8,128)S(1)}, f32[3,2,2,512,512]{3,4,1,0,2:T(8,128)}, u32[]{:S(2)}) copy-start(f32[3,2,2,512,512]{3,4,1,0,2:T(8,128)} %all-gather.21.cloned.1.call-done) | copy-start | bytes 37748740
  350.2 10.7 %copy-start.4 = (f32[1,3,2,512,512]{4,3,2,1,0:T(8,128)S(1)}, f32[1,3,2,512,512]{4,3,2,1,0:T(8,128)}, u32[]{:S(2)}) copy-start(f32[1,3,2,512,512]{4,3,2,1,0:T(8,128)} %all-gather.11.cloned.1.call-done) | copy-start | bytes 18874372
  390.6 4.1 %copy-start.1 = (f32[1,8,2,64,512]{4,3,2,1,0:T(8,128)S(1)}, f32[1,8,2,64,512]{4,3,2,1,0:T(8,128)}, u32[]{:S(2)}) copy-start(f32[1,8,2,64,512]{4,3,2,1,0:T(8,128)} %param.5) | copy-start | bytes 6291460
Sparse Core Ops, SparseCore 0:
  43.4 21.2 all-gather.12
  79.0 36.6 all-gather.14
  117.4 27.3 all-gather.16
  146.3 26.6 all-gather.18
  174.5 71.9 all-gather.10
  248.8 89.9 all-gather.20
where the time goes:
time: 406 us; the launch traced here: 402 us
  waiting for transfers between devices  135 us (33%)
  blocking collectives  130 us (32%)
  matrix products  68.2 us (17%)
  local copies, waits for them, and re-layouts  38.6 us (10%)
  other arithmetic  14.7 us (4%)
  between operations  14.7 us (4%)
    all_gather x16, blocking collectives, all_blocks(): tiles = lax.all_gather(tiles, axes[k], axis=0, tiled=True)  130 us
    all_gather x1, waiting for transfers between devices, per_device(): lax.all_gather(vertex_right, ROW, axis=4, tiled=True)  92.3 us
    all_gather x1, waiting for transfers between devices, per_device(): left_full = lax.all_gather(chosen_left, COL, axis=3, tiled=True)  38.9 us
    dot_general x3, matrix products, complex_product(): jnp.matmul(first_im, second_re, precision=highest)  17 us
    unnamed x4, matrix products  16.6 us
    reshape x3, local copies, waits for them, and re-layouts, all_blocks(): tiles.transpose(*turned, *range(len(order), tiles.ndim))  12.2 us
    dot_general x3, matrix products, complex_product(): jnp.matmul(first_re, second_re, precision=highest)  12.2 us
    dot_general x3, matrix products, complex_product(): jnp.matmul(first_re, second_im, precision=highest)  11.3 us
  transfers between devices with their start and end apart: 6, of which 3 were waited for; matrix products, arithmetic and copies ran while one was open for 16% of the time, Pallas kernels for 0%

commit v1 on v0

--- a/solution.py
+++ b/solution.py
@@ -19,7 +19,9 @@
 def all_blocks(x, axes, order):
     tiles = x[None]
     for k in order:
-        tiles = lax.all_gather(tiles, axes[k], axis=0, tiled=True)
+        tiles = jnp.concatenate(
+            lax.all_to_all(jnp.stack([tiles] * lax.axis_size(axes[k])), axes[k], 0, 0), axis=0
+        )
     held = [lax.axis_size(axes[k]) for k in reversed(order)]
     tiles = tiles.reshape(*held, *x.shape)
     turned = sorted(range(len(order)), key=lambda place: order[len(order) - 1 - place])

time: 406 us -> 496 us (1.22)
  waiting for transfers between devices: 135 us -> 220 us
  blocking collectives: 130 us -> 68.7 us
  starting transfers between devices: 0.21 us -> 59.1 us
  other arithmetic: 14.7 us -> 20.8 us
    all_to_all x0 -> x14, waiting for transfers between devices: none -> 131 us  [all_blocks(): lax.all_to_all(jnp.stack([tiles] * lax.axis_size(axes[k])), axes[k], 0, 0)]
    all_gather x16 -> x0, blocking collectives: 130 us -> none  [all_blocks(): tiles = lax.all_gather(tiles, axes[k], axis=0, tiled=True)]
    all_to_all x0 -> x6, blocking collectives: none -> 68.7 us  [all_blocks(): lax.all_to_all(jnp.stack([tiles] * lax.axis_size(axes[k])), axes[k], 0, 0)]
    all_to_all x0 -> x14, starting transfers between devices: none -> 58.7 us  [all_blocks(): lax.all_to_all(jnp.stack([tiles] * lax.axis_size(axes[k])), axes[k], 0, 0)]
    all_gather x1, waiting for transfers between devices: 38.9 us -> 0.02 us  [per_device(): left_full = lax.all_gather(chosen_left, COL, axis=3, tiled=True)]
    reshape x3 -> x0, local copies, waits for them, and re-layouts: 12.2 us -> none  [all_blocks(): tiles.transpose(*turned, *range(len(order), tiles.ndim))]
    another operation x0 -> x10, local copies, waits for them, and re-layouts: none -> 9.92 us  [the longest x9 7.94 us: all_blocks(): jnp.stack([tiles] * lax.axis_size(axes[k]))]
    another operation x0 -> x12, other arithmetic: none -> 8.09 us  [all_blocks(): jnp.stack([tiles] * lax.axis_size(axes[k]))]
  transfers between devices with their start and end apart: 6 -> 16, of which waited for: 3 -> 15; matrix products, arithmetic and copies ran while one was open for 16% -> 13% of each run, Pallas kernels for 0% -> 0%
where the time goes in v1:
time: 496 us; the launch traced here: 489 us
  waiting for transfers between devices  220 us (44%)
  blocking collectives  68.7 us (14%)
  matrix products  68.2 us (14%)
  starting transfers between devices  59.1 us (12%)
  local copies, waits for them, and re-layouts  37.6 us (8%)
  other arithmetic  20.8 us (4%)
  between operations  14.7 us (3%)
    all_to_all x14, waiting for transfers between devices, all_blocks(): lax.all_to_all(jnp.stack([tiles] * lax.axis_size(axes[k])), axes[k], 0, 0)  131 us
    all_gather x1, waiting for transfers between devices, per_device(): lax.all_gather(vertex_right, ROW, axis=4, tiled=True)  88.4 us
    all_to_all x6, blocking collectives, all_blocks(): lax.all_to_all(jnp.stack([tiles] * lax.axis_size(axes[k])), axes[k], 0, 0)  68.7 us
    all_to_all x14, starting transfers between devices, all_blocks(): lax.all_to_all(jnp.stack([tiles] * lax.axis_size(axes[k])), axes[k], 0, 0)  58.7 us
    dot_general x3, matrix products, complex_product(): jnp.matmul(first_im, second_re, precision=highest)  17 us
    unnamed x4, matrix products  16.6 us
    dot_general x3, matrix products, complex_product(): jnp.matmul(first_re, second_re, precision=highest)  12.2 us
    dot_general x3, matrix products, complex_product(): jnp.matmul(first_re, second_im, precision=highest)  11.3 us
  transfers between devices with their start and end apart: 16, of which 15 were waited for; matrix products, arithmetic and copies ran while one was open for 13% of the time, Pallas kernels for 0%

profile of v1, /device:TPU:1, one launch (start us, length us, event | category | flops | bytes accessed | tf_op | source)
XLA Modules:
  0.0 488.8 jit_solution(10570629052708044330)
XLA Ops:
  14.5 4.6 all-to-all-start.5
  26.2 4.3 all-to-all-start
  30.5 58.7 %all-to-all-done = f32[2,1,3,2,1,512]{5,4,3,2,1,0:T(1,128)S(1)} async-done(((f32[2,1,3,2,1,512]{5,4,3,2,1,0:T(1,128)}), f32[2,1,3,2,1,512]{5,4,3,2,1,0:T(1,128)S(1)}, u32[]{:S(2)}, u32[]{:S(2)}) %all-to-all-start) | async-done | bytes 24608 | tf_op jit(solution)/shard_map/all_to_all | solution.py:23
  89.2 3.9 all_to_all.100
  96.4 4.4 all-to-all-done.6
  101.4 9.4 %all-to-all-start.15 = ((f32[4,1,3,2,1,512]{5,3,2,4,1,0:T(2,128)}), f32[4,1,3,2,1,512]{5,3,2,4,1,0:T(2,128)S(1)}, u32[]{:S(2)}, u32[]{:S(2)}) async-start(f32[4,1,3,2,1,512]{5,3,2,4,1,0:T(2,128)} %stack.111), calls=%async_computation.15 | async-start | bytes 98304 | tf_op jit(solution)/shard_map/all_to_all | solution.py:23
  119.2 4.0 all-to-all-done.12
  130.3 5.5 %all-to-all-start.1 = ((f32[4,2,3,2,1,512]{5,3,2,1,4,0:T(2,128)}), f32[4,2,3,2,1,512]{5,3,2,1,4,0:T(2,128)S(1)}, u32[]{:S(2)}, u32[]{:S(2)}) async-start(f32[4,2,3,2,1,512]{5,3,2,1,4,0:T(2,128)} %stack.97), calls=%async_computation.1 | async-start | bytes 196608 | tf_op jit(solution)/shard_map/all_to_all | solution.py:23
  135.9 4.6 all-to-all-done.1
  140.5 9.9 %all_to_all.101 = f32[2,8,3,2,1,512]{5,3,2,1,4,0:T(2,128)S(1)} all-to-all(f32[2,8,3,2,1,512]{5,3,2,1,4,0:T(2,128)S(1)} %pad_maximum_fusion.5), channel_id=1, replica_groups=mesh['row_0'=4,'row_1'=2,'row_2'=2,'col_0'=2,'col_1'=4] {'row_2'}, dimensions={0} | all-to-all | bytes 393216 | tf_op jit(solution)/shard_map/all_to_all | solution.py:23
  154.6 5.2 %all-to-all-done.7 = f32[4,4,3,2,1,512]{5,3,2,1,4,0:T(2,128)S(1)} async-done(((f32[4,4,3,2,1,512]{5,3,2,1,4,0:T(2,128)}), f32[4,4,3,2,1,512]{5,3,2,1,4,0:T(2,128)S(1)}, u32[]{:S(2)}, u32[]{:S(2)}) %all-to-all-start.7) | async-done | bytes 196640 | tf_op jit(solution)/shard_map/all_to_all | solution.py:23
  159.9 9.0 %all_to_all.102 = f32[2,16,3,2,1,512]{5,3,2,1,4,0:T(2,128)S(1)} all-to-all(f32[2,16,3,2,1,512]{5,3,2,1,4,0:T(2,128)S(1)} %pad_maximum_fusion.4), channel_id=1, replica_groups=mesh['row_0'=4,'row_1'=2,'row_2'=2,'col_0'=2,'col_1'=4] {'row_1'}, dimensions={0} | all-to-all | bytes 786432 | tf_op jit(solution)/shard_map/all_to_all | solution.py:23
  173.3 6.1 %all-to-all-done.2 = f32[4,8,3,2,1,512]{5,3,2,1,4,0:T(2,128)S(1)} async-done(((f32[4,8,3,2,1,512]{5,3,2,1,4,0:T(2,128)}), f32[4,8,3,2,1,512]{5,3,2,1,4,0:T(2,128)S(1)}, u32[]{:S(2)}, u32[]{:S(2)}) %all-to-all-start.2) | async-done | bytes 393248 | tf_op jit(solution)/shard_map/all_to_all | solution.py:23
  184.0 5.9 %all-to-all-done.13 = f32[4,8,3,2,1,512]{5,3,2,1,4,0:T(2,128)S(1)} async-done(((f32[4,8,3,2,1,512]{5,3,2,1,4,0:T(2,128)}), f32[4,8,3,2,1,512]{5,3,2,1,4,0:T(2,128)S(1)}, u32[]{:S(2)}, u32[]{:S(2)}) %all-to-all-start.13) | async-done | bytes 393248 | tf_op jit(solution)/shard_map/all_to_all | solution.py:23
  190.0 10.0 %all_to_all.103 = f32[2,32,3,2,1,512]{5,3,2,1,4,0:T(2,128)} all-to-all(f32[2,32,3,2,1,512]{5,3,2,1,4,0:T(2,128)S(1)} %pad_maximum_fusion.2), channel_id=1, replica_groups=mesh['row_0'=4,'row_1'=2,'row_2'=2,'col_0'=2,'col_1'=4] {'col_0'}, dimensions={0} | all-to-all | bytes 1572864 | tf_op jit(solution)/shard_map/all_to_all | solution.py:23
  206.7 6.2 %all-to-all-done.8 = f32[4,16,3,2,1,512]{5,3,2,1,4,0:T(2,128)S(1)} async-done(((f32[4,16,3,2,1,512]{5,3,2,1,4,0:T(2,128)}), f32[4,16,3,2,1,512]{5,3,2,1,4,0:T(2,128)S(1)}, u32[]{:S(2)}, u32[]{:S(2)}) %all-to-all-start.8) | async-done | bytes 786464 | tf_op jit(solution)/shard_map/all_to_all | solution.py:23
  212.8 12.5 %all_to_all.104 = f32[2,64,3,2,1,512]{5,3,2,1,4,0:T(2,128)} all-to-all(f32[2,64,3,2,1,512]{5,3,2,1,4,0:T(2,128)S(1)} %pad_maximum_fusion), channel_id=1, replica_groups=mesh['row_0'=4,'row_1'=2,'row_2'=2,'col_0'=2,'col_1'=4] {'row_2'}, dimensions={0} | all-to-all | bytes 3145728 | tf_op jit(solution)/shard_map/all_to_all | solution.py:23
  232.1 18.8 %all-to-all-done.14 = f32[4,32,3,2,1,512]{5,3,2,1,4,0:T(2,128)S(1)} async-done(((f32[4,32,3,2,1,512]{5,3,2,1,4,0:T(2,128)}), f32[4,32,3,2,1,512]{5,3,2,1,4,0:T(2,128)S(1)}, u32[]{:S(2)}, u32[]{:S(2)}) %all-to-all-start.14) | async-done | bytes 1572896 | tf_op jit(solution)/shard_map/all_to_all | solution.py:23
  250.8 23.4 %all_to_all.105 = f32[2,64,3,2,1,512]{5,3,2,1,4,0:T(2,128)} all-to-all(f32[2,64,3,2,1,512]{5,3,2,1,4,0:T(2,128)} %pad_maximum_fusion.1), channel_id=1, replica_groups=mesh['row_0'=4,'row_1'=2,'row_2'=2,'col_0'=2,'col_1'=4] {'col_0'}, dimensions={0} | all-to-all | bytes 3145728 | tf_op jit(solution)/shard_map/all_to_all | solution.py:23
  275.8 4.3 all-to-all-start.19
  290.2 8.7 %all-to-all-done.19 = f32[4,32,3,2,1,512]{5,3,2,1,4,0:T(2,128)} async-done(((f32[4,32,3,2,1,512]{5,3,2,1,4,0:T(2,128)}), f32[4,32,3,2,1,512]{5,3,2,1,4,0:T(2,128)}, u32[]{:S(2)}, u32[]{:S(2)}) %all-to-all-start.19) | async-done | bytes 1572896 | tf_op jit(solution)/shard_map/all_to_all | solution.py:23
  298.9 6.0 %maximum_bitcast_fusion = f32[3,2,128,4,512]{4,1,0,2,3:T(2,128)S(1)} fusion(f32[128,3,2,1,512]{4,2,1,0,3:T(2,128)} %bitcast.31, f32[128,3,2,1,512]{4,2,1,0,3:T(2,128)} %bitcast.191, f32[128,3,2,1,512]{4,2,1,0,3:T(2,128)} %bitcast.192, f32[128,3,2,1,512]{4,2,1,0,3:T(2,128)} %bitcast.190), kind=kLoop, calls=%fused_computation.3 | loop fusion | flops 4718592 | bytes 12582912 | tf_op jit(solution)/shard_map/transpose | solution.py:34
  304.9 6.7 %copy.57 = f32[3,2,128,4,512]{4,3,2,0,1:T(4,128)} copy(f32[3,2,128,4,512]{4,1,0,2,3:T(2,128)S(1)} %maximum_bitcast_fusion) | data formatting | bytes 12582912 | tf_op jit(solution)/shard_map/transpose | solution.py:34
  311.6 8.2 %broadcast_in_dim_reshape.3 = f32[3,1,2,512,512]{4,3,0,2,1:T(8,128)} reshape(f32[3,2,128,4,512]{4,3,2,0,1:T(4,128)} %copy.57) | data formatting | bytes 12582912 | tf_op jit(solution)/shard_map/broadcast_in_dim;reshape | solution.py:86
  319.8 5.2 %fusion.3 = f32[3,512,64]{1,2,0:S(1)} fusion(f32[3,512,64]{1,2,0:T(8,128)S(1)} %bitcast.195, f32[3,1,2,512,512]{4,3,0,2,1:T(8,128)} %broadcast_in_dim_reshape.3), kind=kOutput, calls=%fused_computation.10 | convolution fusion | flops 603979776 | bytes 3932160
  325.0 5.0 %fusion.2 = f32[3,512,64]{1,2,0:S(1)} fusion(f32[3,512,64]{1,2,0:T(8,128)S(1)} %bitcast.196, f32[3,1,2,512,512]{4,3,0,2,1:T(8,128)} %broadcast_in_dim_reshape.3), kind=kOutput, calls=%fused_computation.9 | convolution fusion | flops 603979776 | bytes 3932160
  337.5 88.4 %all-gather.5.cloned.1.call-done = f32[3,2,2,512,512]{3,4,1,0,2:T(8,128)} async-done(((f32[3,2,2,512,32]{3,4,1,0,2:T(8,128)}), f32[3,2,2,512,512]{3,4,1,0,2:T(8,128)}) %all-gather.5.cloned.1.call-update) | async-done | bytes 12582928 | tf_op jit(solution)/shard_map/all_gather | solution.py:87
  426.0 5.8 %fusion.13 = f32[512,2,512]{2,0,1:T(8,128)S(1)} fusion(f32[3,2,2,512,512]{3,4,1,0,2:T(8,128)} %all-gather.5.cloned.1.call-done, f32[1,3,2,512,512]{4,3,2,1,0:T(8,128)} %all-gather.3.cloned.1.call-done), kind=kOutput, calls=%fused_computation.32 | convolution fusion | flops 3221225472 | bytes 5242880 | tf_op jit(solution)/shard_map/dot_general | solution.py:54
  431.8 5.5 %fusion.9 = f32[512,2,512]{2,0,1:T(8,128)S(1)} fusion(f32[3,2,2,512,512]{3,4,1,0,2:T(8,128)} %all-gather.5.cloned.1.call-done, f32[1,3,2,512,512]{4,3,2,1,0:T(8,128)} %all-gather.3.cloned.1.call-done), kind=kOutput, calls=%fused_computation.28 | convolution fusion | flops 3221225472 | bytes 5242880 | tf_op jit(solution)/shard_map/dot_general | solution.py:54
  437.3 5.6 %fusion.5 = f32[512,2,512]{2,0,1:T(8,128)S(1)} fusion(f32[3,2,2,512,512]{3,4,1,0,2:T(8,128)} %all-gather.5.cloned.1.call-done, f32[1,3,2,512,512]{4,3,2,1,0:T(8,128)} %all-gather.3.cloned.1.call-done), kind=kOutput, calls=%fused_computation.24 | convolution fusion | flops 3221225472 | bytes 5242880 | tf_op jit(solution)/shard_map/dot_general | solution.py:54
  443.0 5.1 %fusion.14 = f32[512,2,512]{2,0,1:T(8,128)S(1)} fusion(f32[3,2,2,512,512]{3,4,1,0,2:T(8,128)S(1)} %copy-done.3, f32[1,3,2,512,512]{4,3,2,1,0:T(8,128)} %all-gather.3.cloned.1.call-done), kind=kOutput, calls=%fused_computation.33 | convolution fusion | flops 3221225472 | bytes 5242880 | tf_op jit(solution)/shard_map/dot_general | solution.py:51
  458.9 4.0 add_bitcast_fusion.1
  (91 shorter events, 109.0 us)
Async XLA Ops:
  6.5 4.1 copy-start
  6.5 331.0 %all-gather.3.cloned.1.call-start = ((), (), s32[]{:S(2)}) async-start(), calls=%async_computation.20 | async-start | bytes 7077888 | tf_op jit(solution)/shard_map/all_gather | solution.py:85
  14.5 5.7 %all-to-all-start.5 = ((f32[2,1,3,2,1,512]{5,4,3,2,1,0:T(1,128)}), f32[2,1,3,2,1,512]{5,4,3,2,1,0:T(1,128)S(1)}, u32[]{:S(2)}, u32[]{:S(2)}) async-start(f32[2,1,3,2,1,512]{5,4,3,2,1,0:T(1,128)} %pad_maximum_fusion.11), calls=%async_computation.5 | async-start | bytes 49152 | tf_op jit(solution)/shard_map/all_to_all | solution.py:23
  20.2 6.0 %all-to-all-start.10 = ((f32[2,1,3,2,1,512]{5,4,3,2,1,0:T(1,128)}), f32[2,1,3,2,1,512]{5,4,3,2,1,0:T(1,128)S(1)}, u32[]{:S(2)}, u32[]{:S(2)}) async-start(f32[2,1,3,2,1,512]{5,4,3,2,1,0:T(1,128)} %pad_maximum_fusion.12), calls=%async_computation.10 | async-start | bytes 49152 | tf_op jit(solution)/shard_map/all_to_all | solution.py:23
  26.2 63.0 %all-to-all-start = ((f32[2,1,3,2,1,512]{5,4,3,2,1,0:T(1,128)}), f32[2,1,3,2,1,512]{5,4,3,2,1,0:T(1,128)S(1)}, u32[]{:S(2)}, u32[]{:S(2)}) async-start(f32[2,1,3,2,1,512]{5,4,3,2,1,0:T(1,128)} %pad_maximum_fusion.10), calls=%async_computation | async-start | bytes 49152 | tf_op jit(solution)/shard_map/all_to_all | solution.py:23
  93.1 7.7 %all-to-all-start.6 = ((f32[2,2,3,2,1,512]{5,4,3,2,1,0:T(1,128)}), f32[2,2,3,2,1,512]{5,4,3,2,1,0:T(1,128)S(1)}, u32[]{:S(2)}, u32[]{:S(2)}) async-start(f32[2,2,3,2,1,512]{5,4,3,2,1,0:T(1,128)} %pad_maximum_fusion.8), calls=%async_computation.6 | async-start | bytes 98304 | tf_op jit(solution)/shard_map/all_to_all | solution.py:23
  101.4 13.8 %all-to-all-start.15 = ((f32[4,1,3,2,1,512]{5,3,2,4,1,0:T(2,128)}), f32[4,1,3,2,1,512]{5,3,2,4,1,0:T(2,128)S(1)}, u32[]{:S(2)}, u32[]{:S(2)}) async-start(f32[4,1,3,2,1,512]{5,3,2,4,1,0:T(2,128)} %stack.111), calls=%async_computation.15 | async-start | bytes 98304 | tf_op jit(solution)/shard_map/all_to_all | solution.py:23
  115.2 8.0 %all-to-all-start.12 = ((f32[2,4,3,2,1,512]{5,4,3,2,1,0:T(1,128)}), f32[2,4,3,2,1,512]{5,4,3,2,1,0:T(1,128)S(1)}, u32[]{:S(2)}, u32[]{:S(2)}) async-start(f32[2,4,3,2,1,512]{5,4,3,2,1,0:T(1,128)} %pad_maximum_fusion.6), calls=%async_computation.12 | async-start | bytes 196608 | tf_op jit(solution)/shard_map/all_to_all | solution.py:23
  123.2 6.5 %all-to-all-start.16 = ((f32[2,4,3,2,1,512]{5,3,2,1,4,0:T(2,128)}), f32[2,4,3,2,1,512]{5,3,2,1,4,0:T(2,128)S(1)}, u32[]{:S(2)}, u32[]{:S(2)}) async-start(f32[2,4,3,2,1,512]{5,3,2,1,4,0:T(2,128)} %pad_maximum_fusion.7), calls=%async_computation.16 | async-start | bytes 196608 | tf_op jit(solution)/shard_map/all_to_all | solution.py:23
  130.3 10.2 %all-to-all-start.1 = ((f32[4,2,3,2,1,512]{5,3,2,1,4,0:T(2,128)}), f32[4,2,3,2,1,512]{5,3,2,1,4,0:T(2,128)S(1)}, u32[]{:S(2)}, u32[]{:S(2)}) async-start(f32[4,2,3,2,1,512]{5,3,2,1,4,0:T(2,128)} %stack.97), calls=%async_computation.1 | async-start | bytes 196608 | tf_op jit(solution)/shard_map/all_to_all | solution.py:23
  151.1 8.7 %all-to-all-start.7 = ((f32[4,4,3,2,1,512]{5,3,2,1,4,0:T(2,128)}), f32[4,4,3,2,1,512]{5,3,2,1,4,0:T(2,128)S(1)}, u32[]{:S(2)}, u32[]{:S(2)}) async-start(f32[4,4,3,2,1,512]{5,3,2,1,4,0:T(2,128)} %stack.103), calls=%async_computation.7 | async-start | bytes 393216 | tf_op jit(solution)/shard_map/all_to_all | solution.py:23
  169.8 9.7 %all-to-all-start.2 = ((f32[4,8,3,2,1,512]{5,3,2,1,4,0:T(2,128)}), f32[4,8,3,2,1,512]{5,3,2,1,4,0:T(2,128)S(1)}, u32[]{:S(2)}, u32[]{:S(2)}) async-start(f32[4,8,3,2,1,512]{5,3,2,1,4,0:T(2,128)} %stack.98), calls=%async_computation.2 | async-start | bytes 786432 | tf_op jit(solution)/shard_map/all_to_all | solution.py:23
  180.3 9.7 %all-to-all-start.13 = ((f32[4,8,3,2,1,512]{5,3,2,1,4,0:T(2,128)}), f32[4,8,3,2,1,512]{5,3,2,1,4,0:T(2,128)S(1)}, u32[]{:S(2)}, u32[]{:S(2)}) async-start(f32[4,8,3,2,1,512]{5,3,2,1,4,0:T(2,128)} %stack.109), calls=%async_computation.13 | async-start | bytes 786432 | tf_op jit(solution)/shard_map/all_to_all | solution.py:23
  201.0 11.8 %all-to-all-start.8 = ((f32[4,16,3,2,1,512]{5,3,2,1,4,0:T(2,128)}), f32[4,16,3,2,1,512]{5,3,2,1,4,0:T(2,128)S(1)}, u32[]{:S(2)}, u32[]{:S(2)}) async-start(f32[4,16,3,2,1,512]{5,3,2,1,4,0:T(2,128)} %stack.104), calls=%async_computation.8 | async-start | bytes 1572864 | tf_op jit(solution)/shard_map/all_to_all | solution.py:23
  226.9 24.0 %all-to-all-start.14 = ((f32[4,32,3,2,1,512]{5,3,2,1,4,0:T(2,128)}), f32[4,32,3,2,1,512]{5,3,2,1,4,0:T(2,128)S(1)}, u32[]{:S(2)}, u32[]{:S(2)}) async-start(f32[4,32,3,2,1,512]{5,3,2,1,4,0:T(2,128)} %stack.110), calls=%async_computation.14 | async-start | bytes 3145728 | tf_op jit(solution)/shard_map/all_to_all | solution.py:23
  250.8 24.9 %copy-start.6 = (f32[4,32,3,2,1,512]{5,3,2,1,4,0:T(2,128)}, f32[4,32,3,2,1,512]{5,3,2,1,4,0:T(2,128)S(1)}, u32[]{:S(2)}) copy-start(f32[4,32,3,2,1,512]{5,3,2,1,4,0:T(2,128)S(1)} %all-to-all-done.14) | copy-start | bytes 4718596
  275.8 23.1 %all-to-all-start.19 = ((f32[4,32,3,2,1,512]{5,3,2,1,4,0:T(2,128)}), f32[4,32,3,2,1,512]{5,3,2,1,4,0:T(2,128)}, u32[]{:S(2)}, u32[]{:S(2)}) async-start(f32[4,32,3,2,1,512]{5,3,2,1,4,0:T(2,128)} %stack.115), calls=%async_computation.19 | async-start | bytes 3145728 | tf_op jit(solution)/shard_map/all_to_all | solution.py:23
  280.1 145.8 %all-gather.5.cloned.1.call-start = ((), (), s32[]{:S(2)}) async-start(), calls=%async_computation.21 | async-start | bytes 13369344 | tf_op jit(solution)/shard_map/all_gather | solution.py:87
  282.7 1.4 copy-start.5
  283.5 2.6 copy-start.7
  284.1 4.1 copy-start.8
  319.8 10.2 %copy-start.2 = (f32[3,1,2,512,512]{4,3,0,2,1:T(8,128)S(1)}, f32[3,1,2,512,512]{4,3,0,2,1:T(8,128)}, u32[]{:S(2)}) copy-start(f32[3,1,2,512,512]{4,3,0,2,1:T(8,128)} %broadcast_in_dim_reshape.3) | copy-start | bytes 18874372
  426.0 17.0 %copy-start.3 = (f32[3,2,2,512,512]{3,4,1,0,2:T(8,128)S(1)}, f32[3,2,2,512,512]{3,4,1,0,2:T(8,128)}, u32[]{:S(2)}) copy-start(f32[3,2,2,512,512]{3,4,1,0,2:T(8,128)} %all-gather.5.cloned.1.call-done) | copy-start | bytes 37748740
  437.3 10.7 %copy-start.4 = (f32[1,3,2,512,512]{4,3,2,1,0:T(8,128)S(1)}, f32[1,3,2,512,512]{4,3,2,1,0:T(8,128)}, u32[]{:S(2)}) copy-start(f32[1,3,2,512,512]{4,3,2,1,0:T(8,128)} %all-gather.3.cloned.1.call-done) | copy-start | bytes 18874372
  477.7 4.1 copy-start.1
Sparse Core Ops, SparseCore 0:
  12.4 75.2 all-gather.2
  337.6 88.3 all-gather.4
